TPU v7x, 32 devices: a whole 2x2x4 slice. The times are simulated.
32 devices in a mesh: rep: 4 (over y, x), fsdp: 4 (over z), tp: 2 (over core).
Axes of the slice: x: 2, y: 2, z: 4, core: 2. Of those that a mesh axis runs over, the one named last changes fastest.
Arguments:
- hidden: bfloat16 [4096, 4096], P(('rep', 'fsdp')), may hold values from -6 to 6
- norm_gain: float32 [4096], P('fsdp'), may hold values from 0.5 to 1.5
- value_weight: bfloat16 [4096, 1024], P('fsdp', 'tp'), may hold values from -0.09375 to 0.09375
- value_grad: bfloat16 [4096, 1024], P(('rep', 'fsdp'), 'tp'), may hold values from -6 to 6
Outputs:
- input_grad: bfloat16 [4096, 4096], P(('rep', 'fsdp'))
- weight_grad: float32 [4096, 1024], P('fsdp', 'tp')
- gain_grad: float32 [4096], P('fsdp')
All inputs are finite; a program needn't handle non-finite values.
Results may differ from a plain program's by a relative error of at most 0.00125.
Values may be sent and summed in bfloat16 or wider, within the bound.
A program may use at most 64 MiB of HBM per device.

v0:
```python
import jax
import jax.numpy as jnp
from jax import lax
from jax.sharding import PartitionSpec as P

D = 4096
epsilon = 1e-05


def shards(hidden, norm_gain, value_weight, value_grad):
    average = 1.0 / (lax.axis_size("rep") * lax.axis_size("fsdp"))
    inputs = hidden.astype(jnp.float32)
    inv_local = lax.rsqrt(jnp.mean(inputs * inputs, axis=1, keepdims=True) + epsilon)
    columns = lax.all_to_all(hidden, "fsdp", split_axis=1, concat_axis=0, tiled=True)
    inv_rms = lax.all_gather(inv_local, "fsdp", axis=0, tiled=True)
    normal = columns.astype(jnp.float32) * inv_rms
    normed = (normal * norm_gain).astype(jnp.bfloat16)
    group_grad = lax.all_gather(value_grad, "fsdp", axis=0, tiled=True)
    partial_grad = jnp.dot(group_grad, value_weight.T, preferred_element_type=jnp.float32)
    grad_normed = lax.psum(partial_grad, "tp")
    weight_part = jnp.dot(normed.T, group_grad, preferred_element_type=jnp.float32)
    gain_part = jnp.sum(grad_normed * normal, axis=0)
    grad_scaled = grad_normed * norm_gain
    row_total = lax.psum(
        jnp.sum(grad_scaled * normal, axis=1, keepdims=True).astype(jnp.bfloat16), "fsdp"
    ).astype(jnp.float32)
    center = row_total / D
    column_grad = (inv_rms * (grad_scaled - normal * center)).astype(jnp.bfloat16)
    input_grad = lax.all_to_all(column_grad, "fsdp", split_axis=0, concat_axis=1, tiled=True)
    weight_total = lax.psum(weight_part, "rep")
    gain_total = lax.psum(gain_part, "rep")
    return (input_grad, weight_total * average, gain_total * average)


def solution(mesh):
    placed = (P(("rep", "fsdp"), None), P("fsdp"), P("fsdp", "tp"), P(("rep", "fsdp"), "tp"))
    return jax.shard_map(
        shards,
        mesh=mesh,
        in_specs=placed,
        out_specs=(P(("rep", "fsdp"), None), P("fsdp", "tp"), P("fsdp")),
        check_vma=False,
    )
```

profile of v0, /device:TPU:0, one launch (start us, length us, event | category | flops | bytes accessed | tf_op | source)
XLA Modules:
  0.0 209.7 jit_solution(1176009656137438168)
XLA Ops:
  7.2 0.0 copy-start
  7.2 0.0 all-gather.4.cloned.1.call-start
  7.2 0.7 all-gather.4.cloned.1.call-update
  7.9 0.0 all-reduce.3.cloned.1.call-start
  8.0 32.3 %all-gather.4.cloned.1.call-done = bf16[1024,512]{1,0:T(8,128)(2,1)} async-done(((bf16[256,512]{1,0:T(8,128)(2,1)}), bf16[1024,512]{1,0:T(8,128)(2,1)}) %all-gather.4.cloned.1.call-update) | async-done | bytes 1048592 | tf_op jit(solution)/shard_map/all_gather | solution.py:18
  40.3 0.0 copy-done
  40.3 4.5 %fusion = f32[1024,1024]{1,0:T(8,128)} fusion(bf16[1024,512]{1,0:T(8,128)(2,1)} %all-gather.4.cloned.1.call-done, bf16[1024,512]{1,0:T(8,128)(2,1)S(1)} %copy-done), kind=kOutput, calls=%fused_computation.11 | convolution fusion | flops 1073741824 | bytes 6291456 | tf_op jit(solution)/shard_map/dot_general | solution.py:19
  44.8 0.0 copy-start.1
  44.8 0.0 all-reduce.3.cloned.1.call-update
  44.8 1.6 copy-done.1
  46.4 1.5 copy.16
  47.9 0.0 copy-start.2
  47.9 3.8 %all-to-all-start = ((bf16[256,4,1024]{2,0,1:T(8,128)(2,1)}), bf16[256,4,1024]{2,0,1:T(8,128)(2,1)S(1)}, u32[]{:S(2)}, u32[]{:S(2)}) async-start(bf16[256,4,1024]{2,0,1:T(8,128)(2,1)} %bitcast.29), calls=%async_computation | async-start | bytes 4194304 | tf_op jit(solution)/shard_map/all_to_all | solution.py:14
  51.7 2.6 %multiply_reduce_fusion.2 = f32[256]{0:T(256)S(1)} fusion(bf16[256,4096]{1,0:T(8,128)(2,1)} %param.4), kind=kLoop, calls=%fused_computation.5 | loop fusion | flops 3145472 | bytes 2098176 | tf_op jit(solution)/shard_map/reduce_sum | solution.py:13
  54.4 36.9 %all-gather.1 = f32[4,1,256]{2,1,0:T(1,128)S(1)} all-gather(f32[1,1,256]{2,1,0:T(1,128)S(1)} %bitcast.35), channel_id=2, replica_groups=mesh['rep'=4,'fsdp'=4,'tp'=2] {'fsdp'}, dimensions={0}, use_global_device_ids=true | all-gather | bytes 5120 | tf_op jit(solution)/shard_map/all_gather | solution.py:15
  91.3 8.4 %all-to-all-done = bf16[256,4,1024]{2,0,1:T(8,128)(2,1)S(1)} async-done(((bf16[256,4,1024]{2,0,1:T(8,128)(2,1)}), bf16[256,4,1024]{2,0,1:T(8,128)(2,1)S(1)}, u32[]{:S(2)}, u32[]{:S(2)}) %all-to-all-start) | async-done | bytes 2097184 | tf_op jit(solution)/shard_map/all_to_all | solution.py:14
  99.7 0.0 all-reduce.3.cloned.1.call-done
  99.7 0.0 copy-done.2
  99.7 3.3 %multiply_reduce_fusion = (f32[1024]{0:T(1024)S(1)}, bf16[1024]{0:T(1024)(128)(2,1)S(1)}) fusion(f32[1024,1024]{1,0:T(8,128)} %all-reduce.3.cloned.1.call-done, bf16[256,4,1024]{2,0,1:T(8,128)(2,1)S(1)} %all-to-all-done, f32[1024]{0:T(1024)S(1)} %bitcast.32, f32[1024]{0:T(1024)S(1)} %copy-done.2), kind=kLoop, calls=%fused_computation.1 | loop fusion | flops 7337984 | bytes 6305792 | tf_op jit(solution)/shard_map/reduce_sum | solution.py:22
  103.0 11.9 %psum.29 = bf16[1024,1]{0,1:T(2,128)(2,1)S(1)} all-reduce(bf16[1024,1]{0,1:T(2,128)(2,1)S(1)} %convert_element_type.40), channel_id=1, replica_groups=mesh['rep'=4,'fsdp'=4,'tp'=2] {'fsdp'}, use_global_device_ids=true, to_apply=%region_3.0 | all-reduce | flops 1024 | bytes 4096 | tf_op jit(solution)/shard_map/psum | solution.py:24
  115.0 4.3 %multiply_convert_fusion = (bf16[1024,1024]{1,0:T(8,128)(2,1)}, bf16[1024,1024]{1,0:T(8,128)(2,1)}) fusion(bf16[256,4,1024]{2,0,1:T(8,128)(2,1)S(1)} %all-to-all-done, f32[1024]{0:T(1024)S(1)} %bitcast.33, f32[1024]{0:T(1024)S(1)} %copy-done.2, f32[1024]{0:T(1024)S(1)} %bitcast.34, f32[1024,1024]{1,0:T(8,128)} %all-reduce.3.cloned.1.call-done), kind=kLoop, calls=%fused_computation.2 | loop fusion | flops 9437184 | bytes 10498048 | tf_op jit(solution)/shard_map/convert_element_type | solution.py:17
  119.3 3.6 %all-to-all-start.1 = ((bf16[4,256,1024]{2,1,0:T(8,128)(2,1)}), bf16[4,256,1024]{2,1,0:T(8,128)(2,1)S(1)}, u32[]{:S(2)}, u32[]{:S(2)}) async-start(bf16[4,256,1024]{2,1,0:T(8,128)(2,1)} %bitcast.30), calls=%async_computation.1 | async-start | bytes 4194304 | tf_op jit(solution)/shard_map/all_to_all | solution.py:29
  122.9 0.0 all-reduce.5.cloned.1.call-start
  122.9 4.5 %fusion.1 = f32[1024,512]{1,0:T(8,128)} fusion(bf16[1024,1024]{1,0:T(8,128)(2,1)} %get-tuple-element.5, bf16[1024,512]{1,0:T(8,128)(2,1)} %all-gather.4.cloned.1.call-done), kind=kOutput, calls=%fused_computation.12 | convolution fusion | flops 1073741824 | bytes 5242880 | tf_op jit(solution)/shard_map/dot_general | solution.py:21
  127.4 0.0 all-reduce.5.cloned.1.call-update
  127.4 10.0 %psum.31 = f32[1024]{0:T(1024)S(1)} all-reduce(f32[1024]{0:T(1024)S(1)} %get-tuple-element.3), channel_id=1, replica_groups=mesh['rep'=4,'fsdp'=4,'tp'=2] {'rep'}, use_global_device_ids=true, to_apply=%region_6.0 | all-reduce | flops 1024 | bytes 8192 | tf_op jit(solution)/shard_map/psum | solution.py:31
  137.4 0.6 broadcast_multiply_fusion.1
  138.0 60.4 %all-reduce.5.cloned.1.call-done = f32[1024,512]{1,0:T(8,128)} async-done(((f32[1024,512]{1,0:T(8,128)}), f32[1024,512]{1,0:T(8,128)}) %all-reduce.5.cloned.1.call-update) | async-done | bytes 2097168 | tf_op jit(solution)/shard_map/psum | solution.py:30
  198.4 3.1 %broadcast_multiply_fusion = f32[1024,512]{1,0:T(8,128)} fusion(f32[1024,512]{1,0:T(8,128)} %all-reduce.5.cloned.1.call-done), kind=kLoop, calls=%fused_computation.7 | loop fusion | flops 524288 | bytes 4194304 | tf_op jit(solution)/shard_map/mul | solution.py:32
  201.6 0.0 all-to-all-done.1
  201.6 1.6 copy.14
  (3 shorter events, 0.0 us)
Async XLA Ops:
  7.2 33.1 %copy-start = (bf16[1024,512]{1,0:T(8,128)(2,1)S(1)}, bf16[1024,512]{1,0:T(8,128)(2,1)}, u32[]{:S(2)}) copy-start(bf16[1024,512]{1,0:T(8,128)(2,1)} %param.6) | copy-start | bytes 3145732
  7.2 33.1 %all-gather.4.cloned.1.call-start = ((), (), s32[]{:S(2)}) async-start(), calls=%async_computation.2 | async-start | bytes 1310720 | tf_op jit(solution)/shard_map/all_gather | solution.py:18
  7.9 91.8 %all-reduce.3.cloned.1.call-start = ((), (), s32[]{:S(2)}) async-start(), calls=%async_computation.3 | async-start | bytes 8388608 | tf_op jit(solution)/shard_map/psum | solution.py:20
  44.8 1.6 copy-start.1
  47.9 51.8 %copy-start.2 = (f32[1024]{0:T(1024)S(1)}, f32[1024]{0:T(1024)}, u32[]{:S(2)}) copy-start(f32[1024]{0:T(1024)} %param.5) | copy-start | bytes 12292
  47.9 51.8 %all-to-all-start = ((bf16[256,4,1024]{2,0,1:T(8,128)(2,1)}), bf16[256,4,1024]{2,0,1:T(8,128)(2,1)S(1)}, u32[]{:S(2)}, u32[]{:S(2)}) async-start(bf16[256,4,1024]{2,0,1:T(8,128)(2,1)} %bitcast.29), calls=%async_computation | async-start | bytes 4194304 | tf_op jit(solution)/shard_map/all_to_all | solution.py:14
  119.3 82.3 %all-to-all-start.1 = ((bf16[4,256,1024]{2,1,0:T(8,128)(2,1)}), bf16[4,256,1024]{2,1,0:T(8,128)(2,1)S(1)}, u32[]{:S(2)}, u32[]{:S(2)}) async-start(bf16[4,256,1024]{2,1,0:T(8,128)(2,1)} %bitcast.30), calls=%async_computation.1 | async-start | bytes 4194304 | tf_op jit(solution)/shard_map/all_to_all | solution.py:29
  122.9 75.6 %all-reduce.5.cloned.1.call-start = ((), (), s32[]{:S(2)}) async-start(), calls=%async_computation.4 | async-start | bytes 4194304 | tf_op jit(solution)/shard_map/psum | solution.py:30
Sparse Core Ops, SparseCore 0:
  9.6 30.6 all-gather.3
  44.9 27.4 all-reduce.2
  127.6 70.8 all-reduce.4
where the time goes:
time: 210 us
  waiting for transfers between devices  102 us (49%)
  blocking collectives  58.8 us (28%)
  other arithmetic  14 us (7%)
  between operations  13.8 us (7%)
  matrix products  8.97 us (4%)
  starting transfers between devices  7.52 us (4%)
  local copies, waits for them, and re-layouts  4.69 us (2%)
    psum x1, waiting for transfers between devices, shards(): weight_total = lax.psum(weight_part, 'rep')  60.4 us
    all_gather x1, blocking collectives, shards(): inv_rms = lax.all_gather(inv_local, 'fsdp', axis=0, tiled=True)  36.9 us
    all_gather x1, waiting for transfers between devices, shards(): group_grad = lax.all_gather(value_grad, 'fsdp', axis=0, tiled=True)  32.3 us
    psum x1, blocking collectives, shards(): lax.psum(jnp.sum(grad_scaled * normal, axis=1, keepdims=True).astype(jnp....  11.9 us
    psum x1, blocking collectives, shards(): gain_total = lax.psum(gain_part, 'rep')  9.96 us
    all_to_all x1, waiting for transfers between devices, shards(): lax.all_to_all(hidden, 'fsdp', split_axis=1, concat_axis=0, tiled=True)  8.42 us
    dot_general x1, matrix products, shards(): jnp.dot(normed.T, group_grad, preferred_element_type=jnp.float32)  4.49 us
    dot_general x1, matrix products, shards(): jnp.dot(group_grad, value_weight.T, preferred_element_type=jnp.float32)  4.47 us
  transfers between devices with their start and end apart: 5, of which 3 were waited for; matrix products, arithmetic and copies ran while one was open for 6% of the time, Pallas kernels for 0%

commit v1 on v0

--- a/solution.py
+++ b/solution.py
@@ -2,6 +2,7 @@
 import jax.numpy as jnp
 from jax import lax
 from jax.sharding import PartitionSpec as P
+from jax.lax import all_to_all, axis_size
 
 D = 4096
 epsilon = 1e-05
@@ -11,7 +12,13 @@
     average = 1.0 / (lax.axis_size("rep") * lax.axis_size("fsdp"))
     inputs = hidden.astype(jnp.float32)
     inv_local = lax.rsqrt(jnp.mean(inputs * inputs, axis=1, keepdims=True) + epsilon)
-    columns = lax.all_to_all(hidden, "fsdp", split_axis=1, concat_axis=0, tiled=True)
+    high = all_to_all(
+        jnp.stack(jnp.split(hidden, axis_size("fsdp"), axis=1)),
+        concat_axis=0,
+        split_axis=0,
+        axis_name="fsdp",
+    )
+    columns = jnp.concatenate(high, axis=0)
     inv_rms = lax.all_gather(inv_local, "fsdp", axis=0, tiled=True)
     normal = columns.astype(jnp.float32) * inv_rms
     normed = (normal * norm_gain).astype(jnp.bfloat16)

time: 210 us -> 222 us (1.057)
  waiting for transfers between devices: 102 us -> 113 us
    psum x1, waiting for transfers between devices: 60.4 us -> 71.3 us  [shards(): weight_total = lax.psum(weight_part, 'rep')]
  transfers between devices with their start and end apart: 5 -> 5, of which waited for: 3 -> 3; matrix products, arithmetic and copies ran while one was open for 6% -> 5% of each run, Pallas kernels for 0% -> 0%
where the time goes in v1:
time: 222 us
  waiting for transfers between devices  113 us (51%)
  blocking collectives  57.7 us (26%)
  other arithmetic  15.8 us (7%)
  between operations  13.8 us (6%)
  matrix products  8.43 us (4%)
  starting transfers between devices  8.21 us (4%)
  local copies, waits for them, and re-layouts  4.91 us (2%)
    psum x1, waiting for transfers between devices, shards(): weight_total = lax.psum(weight_part, 'rep')  71.3 us
    all_gather x1, blocking collectives, shards(): inv_rms = lax.all_gather(inv_local, 'fsdp', axis=0, tiled=True)  36.8 us
    all_gather x1, waiting for transfers between devices, shards(): group_grad = lax.all_gather(value_grad, 'fsdp', axis=0, tiled=True)  32.3 us
    psum x1, blocking collectives, shards(): lax.psum(jnp.sum(grad_scaled * normal, axis=1, keepdims=True).astype(jnp....  11.9 us
    psum x1, blocking collectives, shards(): gain_total = lax.psum(gain_part, 'rep')  8.9 us
    all_to_all x1, waiting for transfers between devices, shards(): all_to_all(jnp.stack(jnp.split(hidden, axis_size('fsdp'), axis=1)), conca...  8.42 us
    dot_general x1, matrix products, shards(): jnp.dot(group_grad, value_weight.T, preferred_element_type=jnp.float32)  4.47 us
    convert_element_type x1, other arithmetic, shards(): (inv_rms * (grad_scaled - normal * center)).astype(jnp.bfloat16)  4.45 us
  transfers between devices with their start and end apart: 5, of which 3 were waited for; matrix products, arithmetic and copies ran while one was open for 5% of the time, Pallas kernels for 0%

profile of v1, /device:TPU:0, one launch (start us, length us, event | category | flops | bytes accessed | tf_op | source)
XLA Modules:
  0.0 221.6 jit_solution(16710363575894698421)
XLA Ops:
  7.2 0.0 copy-start
  7.2 0.0 all-gather.4.cloned.1.call-start
  7.2 0.7 all-gather.4.cloned.1.call-update
  7.9 0.0 all-reduce.3.cloned.1.call-start
  8.0 32.3 %all-gather.4.cloned.1.call-done = bf16[1024,512]{1,0:T(8,128)(2,1)} async-done(((bf16[256,512]{1,0:T(8,128)(2,1)}), bf16[1024,512]{1,0:T(8,128)(2,1)}) %all-gather.4.cloned.1.call-update) | async-done | bytes 1048592 | tf_op jit(solution)/shard_map/all_gather | solution.py:25
  40.3 0.0 copy-done
  40.3 4.5 %fusion.14 = f32[1024,1024]{1,0:T(8,128)} fusion(bf16[1024,512]{1,0:T(8,128)(2,1)} %all-gather.4.cloned.1.call-done, bf16[1024,512]{1,0:T(8,128)(2,1)S(1)} %copy-done), kind=kOutput, calls=%fused_computation.24 | convolution fusion | flops 1073741824 | bytes 6291456 | tf_op jit(solution)/shard_map/dot_general | solution.py:26
  44.8 0.0 copy-start.1
  44.8 0.0 all-reduce.3.cloned.1.call-update
  44.8 1.6 copy-done.1
  46.4 0.2 slice_bitcast_fusion.3
  46.5 1.6 pad_maximum_fusion
  48.1 3.7 %all-to-all-start = ((bf16[4,256,1024]{2,1,0:T(8,128)(2,1)}), bf16[4,256,1024]{2,1,0:T(8,128)(2,1)S(1)}, u32[]{:S(2)}, u32[]{:S(2)}) async-start(bf16[4,256,1024]{2,1,0:T(8,128)(2,1)} %pad_maximum_fusion), calls=%async_computation | async-start | bytes 4194304 | tf_op jit(solution)/shard_map/all_to_all | solution.py:15
  51.8 0.0 copy-start.2
  51.8 2.7 %multiply_reduce_fusion = f32[256]{0:T(256)S(1)} fusion(bf16[256,4096]{1,0:T(8,128)(2,1)} %param.4), kind=kLoop, calls=%fused_computation.11 | loop fusion | flops 3145472 | bytes 2098176 | tf_op jit(solution)/shard_map/reduce_sum | solution.py:14
  54.5 36.8 %all-gather.1 = f32[4,1,256]{2,1,0:T(1,128)S(1)} all-gather(f32[1,1,256]{2,1,0:T(1,128)S(1)} %bitcast.30), channel_id=2, replica_groups=mesh['rep'=4,'fsdp'=4,'tp'=2] {'fsdp'}, dimensions={0}, use_global_device_ids=true | all-gather | bytes 5120 | tf_op jit(solution)/shard_map/all_gather | solution.py:22
  91.4 8.4 %all-to-all-done = bf16[4,256,1024]{2,1,0:T(8,128)(2,1)S(1)} async-done(((bf16[4,256,1024]{2,1,0:T(8,128)(2,1)}), bf16[4,256,1024]{2,1,0:T(8,128)(2,1)S(1)}, u32[]{:S(2)}, u32[]{:S(2)}) %all-to-all-start) | async-done | bytes 2097184 | tf_op jit(solution)/shard_map/all_to_all | solution.py:15
  99.8 0.0 all-reduce.3.cloned.1.call-done
  99.8 0.0 copy-done.2
  99.8 3.3 %fusion.9 = (f32[1024]{0:T(1024)S(1)}, bf16[1024]{0:T(1024)(128)(2,1)S(1)}) fusion(f32[1024,1024]{1,0:T(8,128)} %all-reduce.3.cloned.1.call-done, bf16[4,256,1024]{2,1,0:T(8,128)(2,1)S(1)} %all-to-all-done, f32[1024]{0:T(1024)S(1)} %bitcast.26, f32[1024]{0:T(1024)S(1)} %copy-done.2), kind=kLoop, calls=%fused_computation.10 | loop fusion | flops 7337984 | bytes 6305792 | tf_op jit(solution)/shard_map/reduce_sum | solution.py:29
  103.1 11.9 %psum.29 = bf16[1024,1]{0,1:T(2,128)(2,1)S(1)} all-reduce(bf16[1024,1]{0,1:T(2,128)(2,1)S(1)} %convert_element_type.36), channel_id=1, replica_groups=mesh['rep'=4,'fsdp'=4,'tp'=2] {'fsdp'}, use_global_device_ids=true, to_apply=%region_3.0 | all-reduce | flops 1024 | bytes 4096 | tf_op jit(solution)/shard_map/psum | solution.py:31
  115.1 4.4 %fusion.7 = bf16[1024,1024]{1,0:T(8,128)(2,1)} fusion(f32[1024,1024]{1,0:T(8,128)} %all-reduce.3.cloned.1.call-done, bf16[4,256,1024]{2,1,0:T(8,128)(2,1)S(1)} %all-to-all-done, f32[1024]{0:T(1024)S(1)} %bitcast.27, f32[1024]{0:T(1024)S(1)} %bitcast.29, f32[1024]{0:T(1024)S(1)} %copy-done.2), kind=kLoop, calls=%fused_computation.8 | loop fusion | flops 7340032 | bytes 8400896 | tf_op jit(solution)/shard_map/convert_element_type | solution.py:35
  119.5 4.4 %all-to-all-start.1 = ((bf16[4,256,1024]{2,1,0:T(8,128)(2,1)}), bf16[4,256,1024]{2,1,0:T(8,128)(2,1)}, u32[]{:S(2)}, u32[]{:S(2)}) async-start(bf16[4,256,1024]{2,1,0:T(8,128)(2,1)} %bitcast.24), calls=%async_computation.1 | async-start | bytes 4194304 | tf_op jit(solution)/shard_map/all_to_all | solution.py:36
  124.0 0.0 all-reduce.5.cloned.1.call-start
  124.0 4.0 %fusion.10 = f32[1024,512]{1,0:T(8,128)} fusion(bf16[1024,512]{1,0:T(8,128)(2,1)} %all-gather.4.cloned.1.call-done, bf16[1024,1024]{1,0:T(8,128)(2,1)S(1)} %bitcast.23, f32[1024]{0:T(1024)S(1)} %bitcast.28, f32[1024]{0:T(1024)S(1)} %copy-done.2), kind=kOutput, calls=%fused_computation.12 | convolution fusion | flops 1077936128 | bytes 5251072 | tf_op jit(solution)/shard_map/dot_general | solution.py:28
  128.0 0.0 all-reduce.5.cloned.1.call-update
  128.0 71.3 %all-reduce.5.cloned.1.call-done = f32[1024,512]{1,0:T(8,128)} async-done(((f32[1024,512]{1,0:T(8,128)}), f32[1024,512]{1,0:T(8,128)}) %all-reduce.5.cloned.1.call-update) | async-done | bytes 2097168 | tf_op jit(solution)/shard_map/psum | solution.py:37
  199.3 3.1 %broadcast_multiply_fusion = f32[1024,512]{1,0:T(8,128)} fusion(f32[1024,512]{1,0:T(8,128)} %all-reduce.5.cloned.1.call-done), kind=kLoop, calls=%fused_computation.16 | loop fusion | flops 524288 | bytes 4194304 | tf_op jit(solution)/shard_map/mul | solution.py:39
  202.5 8.9 %psum.31 = f32[1024]{0:T(1024)S(1)} all-reduce(f32[1024]{0:T(1024)S(1)} %get-tuple-element.3), channel_id=1, replica_groups=mesh['rep'=4,'fsdp'=4,'tp'=2] {'rep'}, use_global_device_ids=true, to_apply=%region_6.0 | all-reduce | flops 1024 | bytes 8192 | tf_op jit(solution)/shard_map/psum | solution.py:38
  211.4 0.6 broadcast_multiply_fusion.1
  212.0 0.0 all-to-all-done.1
  212.0 3.2 %copy.10 = bf16[4,32,8,1024]{3,2,0,1:T(8,128)(2,1)} copy(bf16[4,32,8,1024]{3,2,1,0:T(8,128)(2,1)} %bitcast.11) | data formatting | bytes 4194304 | tf_op jit(solution)/shard_map/all_to_all | solution.py:36
  (3 shorter events, 0.0 us)
Async XLA Ops:
  7.2 33.1 %copy-start = (bf16[1024,512]{1,0:T(8,128)(2,1)S(1)}, bf16[1024,512]{1,0:T(8,128)(2,1)}, u32[]{:S(2)}) copy-start(bf16[1024,512]{1,0:T(8,128)(2,1)} %param.6) | copy-start | bytes 3145732
  7.2 33.1 %all-gather.4.cloned.1.call-start = ((), (), s32[]{:S(2)}) async-start(), calls=%async_computation.2 | async-start | bytes 1310720 | tf_op jit(solution)/shard_map/all_gather | solution.py:25
  7.9 91.9 %all-reduce.3.cloned.1.call-start = ((), (), s32[]{:S(2)}) async-start(), calls=%async_computation.3 | async-start | bytes 8388608 | tf_op jit(solution)/shard_map/psum | solution.py:27
  44.8 1.6 copy-start.1
  48.1 51.7 %all-to-all-start = ((bf16[4,256,1024]{2,1,0:T(8,128)(2,1)}), bf16[4,256,1024]{2,1,0:T(8,128)(2,1)S(1)}, u32[]{:S(2)}, u32[]{:S(2)}) async-start(bf16[4,256,1024]{2,1,0:T(8,128)(2,1)} %pad_maximum_fusion), calls=%async_computation | async-start | bytes 4194304 | tf_op jit(solution)/shard_map/all_to_all | solution.py:15
  51.8 48.0 %copy-start.2 = (f32[1024]{0:T(1024)S(1)}, f32[1024]{0:T(1024)}, u32[]{:S(2)}) copy-start(f32[1024]{0:T(1024)} %param.5) | copy-start | bytes 12292
  119.5 92.4 %all-to-all-start.1 = ((bf16[4,256,1024]{2,1,0:T(8,128)(2,1)}), bf16[4,256,1024]{2,1,0:T(8,128)(2,1)}, u32[]{:S(2)}, u32[]{:S(2)}) async-start(bf16[4,256,1024]{2,1,0:T(8,128)(2,1)} %bitcast.24), calls=%async_computation.1 | async-start | bytes 4194304 | tf_op jit(solution)/shard_map/all_to_all | solution.py:36
  124.0 75.3 %all-reduce.5.cloned.1.call-start = ((), (), s32[]{:S(2)}) async-start(), calls=%async_computation.4 | async-start | bytes 4194304 | tf_op jit(solution)/shard_map/psum | solution.py:37
Sparse Core Ops, SparseCore 0:
  9.6 30.6 all-gather.3
  44.9 27.4 all-reduce.2
  128.5 70.7 all-reduce.4
